TPU v7x, 256 devices: a whole 4x4x8 slice. The times are simulated.
256 devices in a mesh: expert: 16 (over z, core), shard: 16 (over y, x).
Axes of the slice: x: 4, y: 4, z: 8, core: 2. Of those that a mesh axis runs over, the one named last changes fastest.
Arguments:
- w_down: float32 [64, 1024, 2048], P('expert', None, 'shard'), may hold values from -0.25 to 0.25
- avg_down: float32 [64, 1024, 2048], P('expert', None, 'shard'), may hold values from -0.1875 to 0.1875
- mix_share: float32 [64], P('expert'), may hold values from 0.2 to 0.8
- router_weight: float32 [2048, 64], P('shard', 'expert'), may hold values from -0.125 to 0.125
- router_gain: float32 [2048], P('shard'), may hold values from 0.25 to 1.75
Outputs:
- serve_down: bfloat16 [64, 1024, 2048], P('expert')
- scale_down: float32 [64, 1024], P('expert')
- serve_router: bfloat16 [2048, 64], replicated
All inputs are finite; a program needn't handle non-finite values. Where the computation divides by a largest or mean magnitude, that divisor is 1e-20 or more.
Results may differ from a plain program's by a relative error of at most 0.001.
Values may be sent and summed in bfloat16 or wider, within the bound.
No kernel may reach another device: no remote copies, remote signals or barrier semaphores. Data moves between devices by JAX's collectives and lax.ppermute only.
A program may use at most 128 MiB of HBM per device.

v0:
```python
import jax
import jax.numpy as jnp
from jax import lax
from jax.sharding import PartitionSpec as P

D_MODEL = 2048


def sent_to_all(value, axis):
    copies = jnp.broadcast_to(value, (lax.axis_size(axis), *value.shape))
    return lax.all_to_all(copies, axis, split_axis=0, concat_axis=0, tiled=True)


def taken_together(value, axis):
    everything = sent_to_all(value, axis)
    return jnp.sum(everything, axis=0)


def laid_out(tiles, dim):
    shape = list(tiles.shape[1:])
    shape[dim] *= tiles.shape[0]
    return jnp.moveaxis(tiles, 0, dim).reshape(shape)


def gathered_copies(value, axis, dim):
    return laid_out(sent_to_all(value, axis), dim)


def body(w_down, avg_down, mix_share, router_weight, router_gain):
    fresh_down = mix_share[:, None, None] * w_down + (1.0 - mix_share[:, None, None]) * avg_down
    total_down = taken_together(jnp.sum(jnp.abs(fresh_down), axis=2), "shard")
    scale_down = total_down / D_MODEL
    narrow_down = (fresh_down / jnp.expand_dims(scale_down, 2)).astype(jnp.bfloat16)
    serve_down = lax.all_gather(narrow_down, "shard", axis=2, tiled=True)
    part_router = (router_weight * router_gain[:, None]).astype(jnp.bfloat16)
    row_router = gathered_copies(part_router, "shard", 0)
    serve_router = lax.all_gather(row_router, "expert", axis=1, tiled=True)
    return (serve_down, scale_down, serve_router)


def solution(mesh):
    return jax.shard_map(
        body,
        mesh=mesh,
        in_specs=(
            P("expert", None, "shard"),
            P("expert", None, "shard"),
            P("expert"),
            P("shard", "expert"),
            P("shard"),
        ),
        out_specs=(P("expert", None, None), P("expert", None), P()),
        check_vma=False,
    )
```

profile of v0, /device:TPU:2, one launch (start us, length us, event | category | flops | bytes accessed | tf_op | source)
XLA Modules:
  0.0 174.2 jit_solution(17278753643345742411)
XLA Ops:
  7.2 0.0 all-gather.3.cloned.1.call-start
  7.2 0.7 broadcast_subtract_fusion
  7.9 0.0 copy-start
  7.9 0.0 copy-start.2
  7.9 3.1 %abs_reduce_fusion = f32[4,1024]{1,0:T(4,128)S(1)} fusion(f32[4,1024,128]{2,1,0:T(8,128)} %param.6, f32[4]{0:T(128)S(1)} %broadcast_subtract_fusion, f32[4,1024,128]{2,1,0:T(8,128)} %param.5, f32[4]{0:T(128)} %param.7), kind=kLoop, calls=%fused_computation.1 | loop fusion | flops 2617344 | bytes 4210720 | tf_op jit(solution)/shard_map/reduce_sum | solution.py:31
  11.0 14.6 %all_to_all.10 = f32[16,4,1024]{2,1,0:T(4,128)S(1)} all-to-all(f32[16,4,1024]{2,1,0:T(4,128)S(1)} %broadcast_in_dim.4), channel_id=1, replica_groups=mesh['expert'=16,'shard'=16] {'shard'}, dimensions={0} | all-to-all | bytes 524288 | tf_op jit(solution)/shard_map/all_to_all | solution.py:11
  25.6 0.1 reduce_sum.19
  25.7 0.0 copy-done
  25.7 0.0 copy-done.2
  25.7 0.0 copy-start.1
  25.7 0.0 copy-start.3
  25.7 0.0 copy-start.4
  25.7 2.8 %divide_convert_fusion = bf16[4,1024,128]{2,1,0:T(8,128)(2,1)} fusion(f32[4,1024]{1,0:T(4,128)S(1)} %broadcast_multiply_fusion, f32[4,1024,128]{2,1,0:T(8,128)S(1)} %copy-done, f32[4]{0:T(128)S(1)} %broadcast_subtract_fusion, f32[4,1024,128]{2,1,0:T(8,128)} %param.5, f32[4]{0:T(128)S(1)} %copy-done.2), kind=kLoop, calls=%fused_computation | loop fusion | flops 2621440 | bytes 5259296 | tf_op jit(solution)/shard_map/convert_element_type | solution.py:33
  28.5 0.0 copy-done.1
  28.5 0.0 all-gather.3.cloned.1.call-update
  28.5 0.0 copy-done.3
  28.5 0.0 copy-done.4
  28.6 10.5 %all_to_all.11 = bf16[16,128,4]{1,2,0:T(4,128)(2,1)S(1)} all-to-all(bf16[16,128,4]{1,2,0:T(4,128)(2,1)S(1)} %broadcast_in_dim.5), channel_id=1, replica_groups=mesh['expert'=16,'shard'=16] {'shard'}, dimensions={0} | all-to-all | bytes 32768 | tf_op jit(solution)/shard_map/all_to_all | solution.py:11
  39.1 20.7 %all-gather = bf16[16,4,2048]{2,1,0:T(4,128)(2,1)S(1)} all-gather(bf16[1,4,2048]{2,1,0:T(4,128)(2,1)S(1)} %bitcast.7), channel_id=1, replica_groups=mesh['expert'=16,'shard'=16] {'expert'}, dimensions={0}, use_global_device_ids=true | all-gather | bytes 278528 | tf_op jit(solution)/shard_map/all_gather | solution.py:37
  59.7 0.8 reshape.18
  60.5 92.7 %all-gather.3.cloned.1.call-done = bf16[4,1024,2048]{2,1,0:T(8,128)(2,1)} async-done(((bf16[4,1024,128]{2,1,0:T(8,128)(2,1)}), bf16[4,1024,2048]{2,1,0:T(8,128)(2,1)}) %all-gather.3.cloned.1.call-update) | async-done | bytes 16777232 | tf_op jit(solution)/shard_map/all_gather | solution.py:34
  153.2 14.2 %copy.11 = bf16[4,1024,2048]{2,1,0:T(8,128)(2,1)} copy(bf16[4,1024,2048]{2,1,0:T(8,128)(2,1)} %all-gather.3.cloned.1.call-done) | data formatting | bytes 33554432
  (4 shorter events, 0.1 us)
Async XLA Ops:
  7.2 146.0 %all-gather.3.cloned.1.call-start = ((), (), s32[]{:S(2)}) async-start(), calls=%async_computation.2 | async-start | bytes 17825792 | tf_op jit(solution)/shard_map/all_gather | solution.py:34
  7.9 17.8 %copy-start = (f32[4,1024,128]{2,1,0:T(8,128)S(1)}, f32[4,1024,128]{2,1,0:T(8,128)}, u32[]{:S(2)}) copy-start(f32[4,1024,128]{2,1,0:T(8,128)} %param.6) | copy-start | bytes 6291460
  7.9 17.8 %copy-start.2 = (f32[4]{0:T(128)S(1)}, f32[4]{0:T(128)}, u32[]{:S(2)}) copy-start(f32[4]{0:T(128)} %param.7) | copy-start | bytes 52
  25.7 2.8 %copy-start.1 = (f32[4,1024]{1,0:T(4,128)}, f32[4,1024]{1,0:T(4,128)S(1)}, u32[]{:S(2)}) copy-start(f32[4,1024]{1,0:T(4,128)S(1)} %broadcast_multiply_fusion) | copy-start | bytes 49156
  25.7 2.8 %copy-start.3 = (f32[128,4]{0,1:T(4,128)S(1)}, f32[128,4]{0,1:T(4,128)}, u32[]{:S(2)}) copy-start(f32[128,4]{0,1:T(4,128)} %param.8) | copy-start | bytes 6148
  25.7 2.8 %copy-start.4 = (f32[128]{0:T(128)S(1)}, f32[128]{0:T(128)}, u32[]{:S(2)}) copy-start(f32[128]{0:T(128)} %param.9) | copy-start | bytes 1540
Sparse Core Ops, SparseCore 0:
  28.6 124.4 all-gather.2
where the time goes:
time: 174 us
  waiting for transfers between devices  92.7 us (53%)
  blocking collectives  45.8 us (26%)
  local copies, waits for them, and re-layouts  15 us (9%)
  between operations  14.1 us (8%)
  other arithmetic  6.58 us (4%)
    all_gather x1, waiting for transfers between devices, body(): serve_down = lax.all_gather(narrow_down, 'shard', axis=2, tiled=True)  92.7 us
    all_to_all x2, blocking collectives, sent_to_all(): return lax.all_to_all(copies, axis, split_axis=0, concat_axis=0, tiled=True)  25.1 us
    all_gather x1, blocking collectives, body(): serve_router = lax.all_gather(row_router, 'expert', axis=1, tiled=True)  20.7 us
    unnamed x12, local copies, waits for them, and re-layouts  14.9 us
  transfers between devices with their start and end apart: 1, of which 1 were waited for; matrix products, arithmetic and copies ran while one was open for 0% of the time, Pallas kernels for 0%

commit v1 on v0

--- a/solution.py
+++ b/solution.py
@@ -31,7 +31,7 @@
     total_down = taken_together(jnp.sum(jnp.abs(fresh_down), axis=2), "shard")
     scale_down = total_down / D_MODEL
     narrow_down = (fresh_down / jnp.expand_dims(scale_down, 2)).astype(jnp.bfloat16)
-    serve_down = lax.all_gather(narrow_down, "shard", axis=2, tiled=True)
+    serve_down = jnp.concatenate(lax.all_gather(narrow_down, "shard"), axis=2)
     part_router = (router_weight * router_gain[:, None]).astype(jnp.bfloat16)
     row_router = gathered_copies(part_router, "shard", 0)
     serve_router = lax.all_gather(row_router, "expert", axis=1, tiled=True)

time: 174 us -> 168 us (0.966)
  waiting for transfers between devices: 92.7 us -> 84.4 us
    reshape x0 -> x1, local copies, waits for them, and re-layouts: none -> 15.3 us  [body(): serve_down = jnp.concatenate(lax.all_gather(narrow_down, 'shard'), axis=2)]
    unnamed x12 -> x11, local copies, waits for them, and re-layouts: 14.9 us -> 0.79 us
    all_gather x1, waiting for transfers between devices: 92.7 us -> 84.3 us  [body(): serve_down = jnp.concatenate(lax.all_gather(narrow_down, 'shard'), axis=2)]
where the time goes in v1:
time: 168 us; the launch traced here: 167 us
  waiting for transfers between devices  84.4 us (50%)
  blocking collectives  45.8 us (27%)
  local copies, waits for them, and re-layouts  16.2 us (10%)
  between operations  14.1 us (8%)
  other arithmetic  6.58 us (4%)
    all_gather x1, waiting for transfers between devices, body(): serve_down = jnp.concatenate(lax.all_gather(narrow_down, 'shard'), axis=2)  84.3 us
    all_to_all x2, blocking collectives, sent_to_all(): return lax.all_to_all(copies, axis, split_axis=0, concat_axis=0, tiled=True)  25.1 us
    all_gather x1, blocking collectives, body(): serve_router = lax.all_gather(row_router, 'expert', axis=1, tiled=True)  20.7 us
    reshape x1, local copies, waits for them, and re-layouts, body(): serve_down = jnp.concatenate(lax.all_gather(narrow_down, 'shard'), axis=2)  15.3 us
  transfers between devices with their start and end apart: 1, of which 1 were waited for; matrix products, arithmetic and copies ran while one was open for 0% of the time, Pallas kernels for 0%

profile of v1, /device:TPU:2, one launch (start us, length us, event | category | flops | bytes accessed | tf_op | source)
XLA Modules:
  0.0 167.0 jit_solution(15638362901246118198)
XLA Ops:
  7.2 0.0 all-gather.4.cloned.1.call-start
  7.2 0.7 broadcast_subtract_fusion
  7.9 0.0 copy-start
  7.9 0.0 copy-start.2
  7.9 3.1 %abs_reduce_fusion = f32[4,1024]{1,0:T(4,128)S(1)} fusion(f32[4,1024,128]{2,1,0:T(8,128)} %param.6, f32[4]{0:T(128)S(1)} %broadcast_subtract_fusion, f32[4,1024,128]{2,1,0:T(8,128)} %param.5, f32[4]{0:T(128)} %param.7), kind=kLoop, calls=%fused_computation.2 | loop fusion | flops 2617344 | bytes 4210720 | tf_op jit(solution)/shard_map/reduce_sum | solution.py:31
  11.0 14.6 %all_to_all.10 = f32[16,4,1024]{2,1,0:T(4,128)S(1)} all-to-all(f32[16,4,1024]{2,1,0:T(4,128)S(1)} %broadcast_in_dim.4), channel_id=1, replica_groups=mesh['expert'=16,'shard'=16] {'shard'}, dimensions={0} | all-to-all | bytes 524288 | tf_op jit(solution)/shard_map/all_to_all | solution.py:11
  25.6 0.1 reduce_sum.19
  25.7 0.0 copy-done
  25.7 0.0 copy-done.2
  25.7 0.0 copy-start.1
  25.7 0.0 copy-start.3
  25.7 0.0 copy-start.4
  25.7 2.8 %divide_convert_fusion = bf16[4,1024,128]{2,1,0:T(8,128)(2,1)} fusion(f32[4,1024]{1,0:T(4,128)S(1)} %broadcast_multiply_fusion, f32[4,1024,128]{2,1,0:T(8,128)S(1)} %copy-done, f32[4]{0:T(128)S(1)} %broadcast_subtract_fusion, f32[4,1024,128]{2,1,0:T(8,128)} %param.5, f32[4]{0:T(128)S(1)} %copy-done.2), kind=kLoop, calls=%fused_computation.1 | loop fusion | flops 2621440 | bytes 5259296 | tf_op jit(solution)/shard_map/convert_element_type | solution.py:33
  28.5 0.0 copy-done.1
  28.5 0.0 all-gather.4.cloned.1.call-update
  28.5 0.0 copy-done.3
  28.5 0.0 copy-done.4
  28.6 10.5 %all_to_all.11 = bf16[16,128,4]{1,2,0:T(4,128)(2,1)S(1)} all-to-all(bf16[16,128,4]{1,2,0:T(4,128)(2,1)S(1)} %broadcast_in_dim.5), channel_id=1, replica_groups=mesh['expert'=16,'shard'=16] {'shard'}, dimensions={0} | all-to-all | bytes 32768 | tf_op jit(solution)/shard_map/all_to_all | solution.py:11
  39.1 20.7 %all-gather.1 = bf16[16,4,2048]{2,1,0:T(4,128)(2,1)S(1)} all-gather(bf16[1,4,2048]{2,1,0:T(4,128)(2,1)S(1)} %bitcast.16), channel_id=1, replica_groups=mesh['expert'=16,'shard'=16] {'expert'}, dimensions={0}, use_global_device_ids=true | all-gather | bytes 278528 | tf_op jit(solution)/shard_map/all_gather | solution.py:37
  59.7 0.8 reshape.27
  60.5 84.3 %all-gather.4.cloned.1.call-done = bf16[64,1024,128]{2,1,0:T(8,128)(2,1)} async-done(((bf16[4,1024,128]{2,1,0:T(8,128)(2,1)}), bf16[64,1024,128]{2,1,0:T(8,128)(2,1)}) %all-gather.4.cloned.1.call-update) | async-done | bytes 16777232 | tf_op jit(solution)/shard_map/all_gather | solution.py:34
  144.8 15.3 %copy.16 = bf16[16,4,128,8,128]{4,3,0,2,1:T(8,128)(2,1)} copy(bf16[16,4,128,8,128]{4,3,2,1,0:T(8,128)(2,1)} %bitcast.13) | data formatting | bytes 33554432 | tf_op jit(solution)/shard_map/reshape | solution.py:34
  (4 shorter events, 0.1 us)
Async XLA Ops:
  7.2 137.7 %all-gather.4.cloned.1.call-start = ((), (), s32[]{:S(2)}) async-start(), calls=%async_computation.2 | async-start | bytes 17825792 | tf_op jit(solution)/shard_map/all_gather | solution.py:34
  7.9 17.8 %copy-start = (f32[4,1024,128]{2,1,0:T(8,128)S(1)}, f32[4,1024,128]{2,1,0:T(8,128)}, u32[]{:S(2)}) copy-start(f32[4,1024,128]{2,1,0:T(8,128)} %param.6) | copy-start | bytes 6291460
  7.9 17.8 %copy-start.2 = (f32[4]{0:T(128)S(1)}, f32[4]{0:T(128)}, u32[]{:S(2)}) copy-start(f32[4]{0:T(128)} %param.7) | copy-start | bytes 52
  25.7 2.8 %copy-start.1 = (f32[4,1024]{1,0:T(4,128)}, f32[4,1024]{1,0:T(4,128)S(1)}, u32[]{:S(2)}) copy-start(f32[4,1024]{1,0:T(4,128)S(1)} %broadcast_multiply_fusion) | copy-start | bytes 49156
  25.7 2.8 %copy-start.3 = (f32[128,4]{0,1:T(4,128)S(1)}, f32[128,4]{0,1:T(4,128)}, u32[]{:S(2)}) copy-start(f32[128,4]{0,1:T(4,128)} %param.8) | copy-start | bytes 6148
  25.7 2.8 %copy-start.4 = (f32[128]{0:T(128)S(1)}, f32[128]{0:T(128)}, u32[]{:S(2)}) copy-start(f32[128]{0:T(128)} %param.9) | copy-start | bytes 1540
Sparse Core Ops, SparseCore 0:
  28.6 116.1 all-gather.3
